TPU v7x, 8 devices: a whole 2x2x1 slice. The times are simulated.
8 devices in a mesh: rep: 1 (over z), tp: 2 (over y), sp: 4 (over x, core).
Axes of the slice: x: 2, y: 2, z: 1, core: 2. Of those that a mesh axis runs over, the one named last changes fastest.
Arguments:
- x_tokens: bfloat16 [8192, 3840], P(('rep', 'sp'))
- positions: int32 [8192], P(('rep', 'sp'))
- gains: float32 [2, 4, 3840], replicated
- w_q: bfloat16 [2, 3840, 16, 256], P(None, None, 'tp')
- w_k: bfloat16 [2, 3840, 8, 256], P(None, None, 'tp')
- w_v: bfloat16 [2, 3840, 8, 256], P(None, None, 'tp')
- w_o: bfloat16 [2, 16, 256, 3840], P(None, 'tp')
- w_gate: bfloat16 [2, 3840, 15360], P(None, None, 'tp')
- w_up: bfloat16 [2, 3840, 15360], P(None, None, 'tp')
- w_down: bfloat16 [2, 15360, 3840], P(None, 'tp')
Outputs:
- output 1: bfloat16 [8192, 3840], P(('rep', 'sp'))
- output 2: bfloat16 [512, 8, 256], P('rep', ('tp', 'sp'))
- output 3: bfloat16 [512, 8, 256], P('rep', ('tp', 'sp'))
- output 4: bfloat16 [8192, 8, 256], P('rep', ('tp', 'sp'))
- output 5: bfloat16 [8192, 8, 256], P('rep', ('tp', 'sp'))
All inputs are finite; a program needn't handle non-finite values.
Results may differ from a plain program's by a relative error of at most 0.0163675.
Values are sent between devices in bfloat16 or wider.
A program may use at most 2 GiB of HBM per device.

v0:
```python
import jax
import jax.numpy as jnp
from jax import lax
from jax.sharding import PartitionSpec as P, NamedSharding

NORM_EPS = 1e-6
WINDOW = 512
Q_BLOCK = 256
LOCAL_BASE = 10000.0
GLOBAL_BASE = 1000000.0


def rms_norm(values, gain):
    wide = values.astype(jnp.float32)
    inv_rms = lax.rsqrt(jnp.mean(wide * wide, axis=-1, keepdims=True) + NORM_EPS)
    return wide * inv_rms * gain


def rotary(projected, positions, base):
    half = projected.shape[-1] // 2
    inv_freq = base ** (-jnp.arange(half, dtype=jnp.float32) / half)
    angles = positions.astype(jnp.float32)[..., None] * inv_freq
    cos_part = jnp.cos(angles)[..., None, :]
    sin_part = jnp.sin(angles)[..., None, :]
    first = projected[..., :half]
    second = projected[..., half:]
    return jnp.concatenate([first * cos_part - second * sin_part, second * cos_part + first * sin_part], axis=-1)


def attend(q_heads, k_heads, v_heads, q_first, local):
    total = k_heads.shape[0]
    span = WINDOW + Q_BLOCK if local else total
    scale = q_heads.shape[-1] ** -0.5

    def one_block(block_id):
        q_start = block_id * Q_BLOCK
        q_tile = lax.dynamic_slice_in_dim(q_heads, q_start, Q_BLOCK, 0)
        q_idx = q_first + q_start + jnp.arange(Q_BLOCK)
        k_start = jnp.clip(q_first + q_start - WINDOW, 0, total - span) if local else 0
        k_tile = lax.dynamic_slice_in_dim(k_heads, k_start, span, 0)
        v_tile = lax.dynamic_slice_in_dim(v_heads, k_start, span, 0)
        k_idx = k_start + jnp.arange(span)
        allowed = k_idx[None, :] <= q_idx[:, None]
        if local:
            allowed = allowed & (q_idx[:, None] - k_idx[None, :] < WINDOW)
        scores = jnp.einsum('qhgd,khd->hgqk', q_tile, k_tile, preferred_element_type=jnp.float32) * scale
        weights = jax.nn.softmax(jnp.where(allowed, scores, -1e30), axis=-1).astype(jnp.bfloat16)
        return jnp.einsum('hgqk,khd->qhgd', weights, v_tile, preferred_element_type=jnp.float32).astype(jnp.bfloat16)

    blocks = lax.map(one_block, jnp.arange(q_heads.shape[0] // Q_BLOCK))
    return blocks.reshape(q_heads.shape)


def solution(mesh):
    sp_size = mesh.shape['sp']

    def layer(x_loc, pos_loc, gain, w_q, w_k, w_v, w_o, w_gate, w_up, w_down, local):
        base = LOCAL_BASE if local else GLOBAL_BASE
        u_norm = rms_norm(x_loc, gain[0]).astype(jnp.bfloat16)
        q_rot = rotary(jnp.einsum('td,dhe->the', u_norm, w_q, preferred_element_type=jnp.float32), pos_loc, base).astype(jnp.bfloat16)
        k_rot = rotary(jnp.einsum('td,dhe->the', u_norm, w_k, preferred_element_type=jnp.float32), pos_loc, base).astype(jnp.bfloat16)
        v_new = jnp.einsum('td,dhe->the', u_norm, w_v, preferred_element_type=jnp.float32).astype(jnp.bfloat16)
        seq_dev, heads_tp, head_dim = q_rot.shape
        kv_tp = k_rot.shape[1]
        heads_dev = heads_tp // sp_size
        cache_dev = max(kv_tp // sp_size, 1)
        repeat = sp_size * cache_dev // kv_tp
        outgoing = jnp.concatenate([
            q_rot.reshape(seq_dev, sp_size, heads_dev, head_dim),
            jnp.repeat(k_rot, repeat, axis=1).reshape(seq_dev, sp_size, cache_dev, head_dim),
            jnp.repeat(v_new, repeat, axis=1).reshape(seq_dev, sp_size, cache_dev, head_dim)], axis=2)
        received = lax.all_to_all(outgoing, 'sp', 1, 0, tiled=True)
        total = received.shape[0]
        received = received.reshape(total, heads_dev + 2 * cache_dev, head_dim)
        q_all = received[:, :heads_dev].reshape(total, cache_dev, heads_dev // cache_dev, head_dim)
        k_all = received[:, heads_dev:heads_dev + cache_dev]
        v_all = received[:, heads_dev + cache_dev:]
        attn_out = attend(q_all, k_all, v_all, 0, local).reshape(sp_size, seq_dev, heads_dev, head_dim)
        attn_back = lax.all_to_all(attn_out, 'sp', 0, 2, tiled=True).reshape(seq_dev, heads_tp, head_dim)
        o_sum = lax.psum(jnp.einsum('the,hed->td', attn_back, w_o, preferred_element_type=jnp.float32), 'tp')
        x_mid = (x_loc.astype(jnp.float32) + rms_norm(o_sum, gain[1])).astype(jnp.bfloat16)
        u_mlp = rms_norm(x_mid, gain[2]).astype(jnp.bfloat16)
        gate_pre = jnp.dot(u_mlp, w_gate, preferred_element_type=jnp.float32)
        up_pre = jnp.dot(u_mlp, w_up, preferred_element_type=jnp.float32)
        hidden_act = (jax.nn.silu(gate_pre) * up_pre).astype(jnp.bfloat16)
        m_sum = lax.psum(jnp.dot(hidden_act, w_down, preferred_element_type=jnp.float32), 'tp')
        x_out = (x_mid.astype(jnp.float32) + rms_norm(m_sum, gain[3])).astype(jnp.bfloat16)
        if local:
            return x_out, k_all[total - WINDOW:], v_all[total - WINDOW:]
        return x_out, k_all, v_all

    def device_fn(x_loc, pos_loc, gains, w_q, w_k, w_v, w_o, w_gate, w_up, w_down):
        hidden, k_local, v_local = layer(x_loc, pos_loc, gains[0], w_q[0], w_k[0], w_v[0], w_o[0], w_gate[0], w_up[0], w_down[0], True)
        out_hidden, k_global, v_global = layer(hidden, pos_loc, gains[1], w_q[1], w_k[1], w_v[1], w_o[1], w_gate[1], w_up[1], w_down[1], False)
        return out_hidden, k_local, v_local, k_global, v_global

    token_spec = P(('rep', 'sp'), None)
    cache_spec = P('rep', ('tp', 'sp'), None)
    in_specs = (token_spec, P(('rep', 'sp')), P(), P(None, None, 'tp', None), P(None, None, 'tp', None),
                P(None, None, 'tp', None), P(None, 'tp', None, None), P(None, None, 'tp'), P(None, None, 'tp'),
                P(None, 'tp', None))
    out_specs = (token_spec, cache_spec, cache_spec, cache_spec, cache_spec)
    return jax.shard_map(device_fn, mesh=mesh, in_specs=in_specs, out_specs=out_specs, check_vma=False)
```

profile of v0, /device:TPU:0, one launch (start us, length us, event | category | flops | bytes accessed | tf_op | source)
XLA Modules:
  0.0 6017.8 jit_solution(9217579427344919240)
XLA Ops:
  146.2 41.3 fusion.75
  227.2 183.7 %all-to-all-done = bf16[2048,4,4,256]{0,3,2,1:T(8,128)(2,1)} async-done(((bf16[2048,4,4,256]{0,3,2,1:T(8,128)(2,1)}), bf16[2048,4,4,256]{0,3,2,1:T(8,128)(2,1)}, u32[]{:S(2)}, u32[]{:S(2)}) %all-to-all-start) | async-done | bytes 16777248 | tf_op jit(solution)/shard_map/all_to_all | solution.py:72
  410.9 22.1 copy.55
  450.2 184.9 %while.22 = (s32[]{:T(128)}, bf16[32,256,1,2,256]{4,1,0,3,2:T(8,128)(2,1)}, s32[32]{0:T(128)S(1)}, bf16[8192,1,256]{2,0,1:T(8,128)(2,1)}, bf16[8192,1,256]{2,0,1...) while((s32[]{:T(128)}, ...), condition=%wide.region_4.5_spmd, body=%wide.region_1.4_spmd.sunk | while | flops 406716416 | bytes 7489779 | solution.py:50
  642.3 97.0 %all_to_all.60 = bf16[4,2048,2,256]{3,1,2,0:T(8,128)(2,1)S(1)} all-to-all(bf16[4,2048,2,256]{3,1,2,0:T(8,128)(2,1)} %copy.59), channel_id=1, replica_groups=mesh['rep'=1,'tp'=2,'sp'=4] {'sp'}, dimensions={0} | all-to-all | bytes 16777216 | tf_op jit(solution)/shard_map/all_to_all | solution.py:79
  739.3 39.3 convolution_bitcast_fusion.1
  778.7 687.9 %all-reduce.5.cloned.1.call-done = f32[2048,3840]{1,0:T(8,128)} async-done(((f32[2048,3840]{1,0:T(8,128)}), f32[2048,3840]{1,0:T(8,128)}) %all-reduce.5.cloned.1.call-update) | async-done | bytes 31457296 | tf_op jit(solution)/shard_map/psum | solution.py:80
  1502.0 136.8 %fusion.43 = f32[2048,7680]{1,0:T(8,128)} fusion(bf16[2,3840,7680]{2,1,0:T(8,128)(2,1)} %param.22, bf16[2048,3840]{1,0:T(8,128)(2,1)} %get-tuple-element.171, f32[3840]{0:T(1024)S(1)} %copy-done.20, f32[2048]{0:T(1024)S(1)} %add_rsqrt_fusion.5), kind=kOutput, calls=%fused_computation.46 | convolution fusion | flops 120827412480 | bytes 137649152 | tf_op jit(solution)/shard_map/dot_general | solution.py:84
  1638.8 136.9 %fusion.45 = f32[2048,7680]{1,0:T(8,128)} fusion(bf16[2,3840,7680]{2,1,0:T(8,128)(2,1)} %param.21, bf16[2048,3840]{1,0:T(8,128)(2,1)} %get-tuple-element.171, f32[3840]{0:T(1024)S(1)} %copy-done.20, f32[2048]{0:T(1024)S(1)} %add_rsqrt_fusion.5), kind=kOutput, calls=%fused_computation.48 | convolution fusion | flops 120827412480 | bytes 137649152 | tf_op jit(solution)/shard_map/dot_general | solution.py:83
  1775.7 150.1 %fusion.41 = f32[2048,3840]{1,0:T(8,128)} fusion(bf16[2,7680,3840]{2,1,0:T(8,128)(2,1)} %param.23, f32[2048,7680]{1,0:T(8,128)} %fusion.43, f32[2048,7680]{1,0:T(8,128)} %fusion.45), kind=kOutput, calls=%fused_computation.44 | convolution fusion | flops 120890327040 | bytes 216268800 | tf_op jit(solution)/shard_map/dot_general | solution.py:86
  1959.4 653.6 %all-reduce.7.cloned.1.call-done = f32[2048,3840]{1,0:T(8,128)} async-done(((f32[2048,3840]{1,0:T(8,128)}), f32[2048,3840]{1,0:T(8,128)}) %all-reduce.7.cloned.1.call-update) | async-done | bytes 31457296 | tf_op jit(solution)/shard_map/psum | solution.py:86
  2648.3 23.1 convert_bitcast_fusion
  2677.5 23.7 fusion.81
  2701.2 41.2 fusion.72
  2768.8 182.7 %all-to-all-done.2 = bf16[2048,4,4,256]{0,3,2,1:T(8,128)(2,1)} async-done(((bf16[2048,4,4,256]{0,3,2,1:T(8,128)(2,1)}), bf16[2048,4,4,256]{0,3,2,1:T(8,128)(2,1)}, u32[]{:S(2)}, u32[]{:S(2)}) %all-to-all-start.2) | async-done | bytes 16777248 | tf_op jit(solution)/shard_map/all_to_all | solution.py:72
  2951.4 21.7 copy.65
  2990.3 1010.3 %while.23 = (s32[]{:T(128)}, bf16[32,256,1,2,256]{4,1,0,3,2:T(8,128)(2,1)}, s32[32]{0:T(128)S(1)}, bf16[8192,1,2,256]{3,0,2,1:T(8,128)(2,1)}, bf16[8192,1,256]{2...) while((s32[]{:T(128)}, ...), condition=%wide.region_14.15_spmd, body=%wide.region_11.14_spmd.sunk | while | flops 4330748928 | bytes 80228552 | solution.py:50
  4007.8 97.0 %all_to_all.61 = bf16[4,2048,2,256]{3,1,2,0:T(8,128)(2,1)S(1)} all-to-all(bf16[4,2048,2,256]{3,1,2,0:T(8,128)(2,1)} %copy.67), channel_id=1, replica_groups=mesh['rep'=1,'tp'=2,'sp'=4] {'sp'}, dimensions={0} | all-to-all | bytes 16777216 | tf_op jit(solution)/shard_map/all_to_all | solution.py:79
  4104.7 39.3 convolution_bitcast_fusion
  4144.2 686.0 %all-reduce.9.cloned.1.call-done = f32[2048,3840]{1,0:T(8,128)} async-done(((f32[2048,3840]{1,0:T(8,128)}), f32[2048,3840]{1,0:T(8,128)}) %all-reduce.9.cloned.1.call-update) | async-done | bytes 31457296 | tf_op jit(solution)/shard_map/psum | solution.py:80
  4865.5 136.8 %fusion.37 = f32[2048,7680]{1,0:T(8,128)} fusion(bf16[2,3840,7680]{2,1,0:T(8,128)(2,1)} %param.22, bf16[2048,3840]{1,0:T(8,128)(2,1)} %get-tuple-element.167, f32[3840]{0:T(1024)S(1)} %copy-done.18, f32[2048]{0:T(1024)S(1)} %add_rsqrt_fusion.1), kind=kOutput, calls=%fused_computation.40 | convolution fusion | flops 120827412480 | bytes 137649152 | tf_op jit(solution)/shard_map/dot_general | solution.py:84
  5002.3 136.9 %fusion.39 = f32[2048,7680]{1,0:T(8,128)} fusion(bf16[2,3840,7680]{2,1,0:T(8,128)(2,1)} %param.21, bf16[2048,3840]{1,0:T(8,128)(2,1)} %get-tuple-element.167, f32[3840]{0:T(1024)S(1)} %copy-done.18, f32[2048]{0:T(1024)S(1)} %add_rsqrt_fusion.1), kind=kOutput, calls=%fused_computation.42 | convolution fusion | flops 120827412480 | bytes 137649152 | tf_op jit(solution)/shard_map/dot_general | solution.py:83
  5139.2 149.8 %fusion.35 = f32[2048,3840]{1,0:T(8,128)} fusion(bf16[2,7680,3840]{2,1,0:T(8,128)(2,1)} %param.23, f32[2048,7680]{1,0:T(8,128)} %fusion.37, f32[2048,7680]{1,0:T(8,128)} %fusion.39), kind=kOutput, calls=%fused_computation.38 | convolution fusion | flops 120890327040 | bytes 216268800 | tf_op jit(solution)/shard_map/dot_general | solution.py:86
  5291.0 685.2 %all-reduce.11.cloned.1.call-done = f32[2048,3840]{1,0:T(8,128)} async-done(((f32[2048,3840]{1,0:T(8,128)}), f32[2048,3840]{1,0:T(8,128)}) %all-reduce.11.cloned.1.call-update) | async-done | bytes 31457296 | tf_op jit(solution)/shard_map/psum | solution.py:86
  (658 shorter events, 1587.5 us)
Async XLA Ops:
  39.5 38.1 slice-start
  55.9 21.7 slice-start.1
  55.9 21.7 slice-start.2
  55.9 21.7 slice-start.3
  146.2 41.3 copy-start.17
  146.2 41.3 copy-start.21
  146.2 41.3 copy-start.22
  220.2 190.8 %all-to-all-start = ((bf16[2048,4,4,256]{0,3,2,1:T(8,128)(2,1)}), bf16[2048,4,4,256]{0,3,2,1:T(8,128)(2,1)}, u32[]{:S(2)}, u32[]{:S(2)}) async-start(bf16[2048,4,4,256]{0,3,2,1:T(8,128)(2,1)} %pad_maximum_fusion), calls=%async_computation | async-start | bytes 33554432 | tf_op jit(solution)/shard_map/all_to_all | solution.py:72
  227.1 1239.4 %all-reduce.5.cloned.1.call-start = ((), (), s32[]{:S(2)}) async-start(), calls=%async_computation.4 | async-start | bytes 62914560 | tf_op jit(solution)/shard_map/psum | solution.py:80
  778.6 700.4 %copy-start.16 = (f32[3840]{0:T(1024)S(1)}, f32[3840]{0:T(1024)}, u32[]{:S(2)}) copy-start(f32[3840]{0:T(1024)} %get-tuple-element.139) | copy-start | bytes 46084
  778.6 1834.3 %all-reduce.7.cloned.1.call-start = ((), (), s32[]{:S(2)}) async-start(), calls=%async_computation.5 | async-start | bytes 62914560 | tf_op jit(solution)/shard_map/psum | solution.py:86
  1466.5 19.0 copy-start.3
  1485.5 16.5 copy-start.20
  1959.4 666.1 %copy-start.15 = (f32[3840]{0:T(1024)S(1)}, f32[3840]{0:T(1024)}, u32[]{:S(2)}) copy-start(f32[3840]{0:T(1024)} %get-tuple-element.137) | copy-start | bytes 46084
  2612.9 19.0 copy-start
  2701.2 41.2 copy-start.8
  2701.2 41.2 copy-start.9
  2761.8 189.7 %all-to-all-start.2 = ((bf16[2048,4,4,256]{0,3,2,1:T(8,128)(2,1)}), bf16[2048,4,4,256]{0,3,2,1:T(8,128)(2,1)}, u32[]{:S(2)}, u32[]{:S(2)}) async-start(bf16[2048,4,4,256]{0,3,2,1:T(8,128)(2,1)} %pad_maximum_fusion.1), calls=%async_computation.2 | async-start | bytes 33554432 | tf_op jit(solution)/shard_map/all_to_all | solution.py:72
  2768.7 2061.4 %all-reduce.9.cloned.1.call-start = ((), (), s32[]{:S(2)}) async-start(), calls=%async_computation.6 | async-start | bytes 62914560 | tf_op jit(solution)/shard_map/psum | solution.py:80
  4144.1 698.5 %copy-start.14 = (f32[3840]{0:T(1024)S(1)}, f32[3840]{0:T(1024)}, u32[]{:S(2)}) copy-start(f32[3840]{0:T(1024)} %get-tuple-element.135) | copy-start | bytes 46084
  4144.1 1832.1 %all-reduce.11.cloned.1.call-start = ((), (), s32[]{:S(2)}) async-start(), calls=%async_computation.7 | async-start | bytes 62914560 | tf_op jit(solution)/shard_map/psum | solution.py:86
  4830.1 19.0 copy-start.2
  5290.9 697.8 %copy-start.13 = (f32[3840]{0:T(1024)S(1)}, f32[3840]{0:T(1024)}, u32[]{:S(2)}) copy-start(f32[3840]{0:T(1024)} %get-tuple-element.134) | copy-start | bytes 46084
  5976.2 19.0 copy-start.1
  (40 other events, 364.5 us)
Sparse Core Ops, SparseCore 0:
  778.7 687.7 all-reduce.4
  1925.9 686.9 all-reduce.6
  4144.2 685.8 all-reduce.8
  5289.2 686.9 all-reduce.10
where the time goes:
time: 6030 us; the launch traced here: 6020 us
  waiting for transfers between devices  3080 us (51%)
  matrix products  1860 us (31%)
  other arithmetic  497 us (8%)
  local copies, waits for them, and re-layouts  314 us (5%)
  blocking collectives  194 us (3%)
    psum x2, waiting for transfers between devices, layer(): lax.psum(jnp.einsum('the,hed->td', attn_back, w_o, preferred_element_type...  1370 us
    psum x2, waiting for transfers between devices, layer(): lax.psum(jnp.dot(hidden_act, w_down, preferred_element_type=jnp.float32),...  1340 us
    dot_general x64, matrix products, one_block(): jnp.einsum('qhgd,khd->hgqk', q_tile, k_tile, preferred_element_type=jnp.f...  417 us
    all_to_all x2, waiting for transfers between devices, layer(): received = lax.all_to_all(outgoing, 'sp', 1, 0, tiled=True)  366 us
    dot_general x64, matrix products, one_block(): jnp.einsum('hgqk,khd->qhgd', weights, v_tile, preferred_element_type=jnp....  347 us
    dot_general x2, matrix products, layer(): jnp.dot(hidden_act, w_down, preferred_element_type=jnp.float32)  300 us
    dot_general x2, matrix products, layer(): gate_pre = jnp.dot(u_mlp, w_gate, preferred_element_type=jnp.float32)  274 us
    dot_general x2, matrix products, layer(): up_pre = jnp.dot(u_mlp, w_up, preferred_element_type=jnp.float32)  274 us
  transfers between devices with their start and end apart: 6, of which 6 were waited for; matrix products, arithmetic and copies ran while one was open for 1% of the time, Pallas kernels for 0%

commit v1 on v0

v1 whole, which is shorter than its diff:
```python
import functools
import math

import jax
import jax.numpy as jnp
from jax import lax
from jax.experimental import pallas as pl
from jax.experimental.pallas import tpu as pltpu
from jax.sharding import PartitionSpec as P


NORM_EPS = 1e-6
WINDOW = 512
LOCAL_BASE = 10000.0
GLOBAL_BASE = 1000000.0
CHUNK = 512
HALF = CHUNK // 2
HEAD = 256
NEG = -1e30
VMEM = 62 * 1024 * 1024
BF16 = jnp.bfloat16
F32 = jnp.float32


def cost(flops, nbytes):
    return pl.CostEstimate(flops=int(flops), bytes_accessed=int(nbytes), transcendentals=0)


def call(kernel, grid, in_specs, out_specs, out_shape, args, scalars=(), scratch=(), after=(), aliases=None, cost_estimate=None):
    first = len(scalars) + len(in_specs)
    extra = len(after)
    wrapped = lambda *refs: kernel(*refs[:first], *refs[first + extra:])
    return pl.pallas_call(
        wrapped,
        grid_spec=pltpu.PrefetchScalarGridSpec(
            num_scalar_prefetch=len(scalars), grid=grid, in_specs=list(in_specs) + [pl.BlockSpec(memory_space=pl.ANY)] * extra,
            out_specs=out_specs, scratch_shapes=scratch),
        out_shape=out_shape, cost_estimate=cost_estimate, input_output_aliases=aliases or {},
        compiler_params=pltpu.CompilerParams(dimension_semantics=('arbitrary',) * len(grid), vmem_limit_bytes=VMEM))(
            *scalars, *args, *after)


LANES = 128


def tiles(width):
    return [slice(i * LANES, (i + 1) * LANES) for i in range(width // LANES)]


def row_blocks(rows, size, fn):
    def body(i, carry):
        fn(pl.multiple_of(i * size, size))
        return carry

    lax.fori_loop(0, rows // size, body, 0)


def to_inv_rms(sums_ref, rows, width):
    mean = jnp.sum(sums_ref[:rows], axis=1, keepdims=True) * (1.0 / width)
    sums_ref[:rows] = jnp.broadcast_to(lax.rsqrt(mean + NORM_EPS), (rows, LANES))


REGROUP_ROWS = 128


def regroup_kernel(q_ref, k_ref, v_ref, o_ref):
    def pick(heads):
        depth = HEAD // heads
        row = lax.broadcasted_iota(jnp.int32, (HEAD, HEAD), 0)
        col = lax.broadcasted_iota(jnp.int32, (HEAD, HEAD), 1)
        return (lax.rem(row, depth) * heads + row // depth == col).astype(BF16)

    rows = o_ref.shape[0]
    groups = k_ref.shape[2]
    per = q_ref.shape[2] // groups
    width = (per + 2) * HEAD
    for ref, first, count in ((q_ref, 0, per), (k_ref, per, 1), (v_ref, per + 1, 1)):
        heads = groups * count
        depth = HEAD // heads
        order = pick(heads)
        for b in range(rows // depth):
            block = ref[0, b * depth:(b + 1) * depth].reshape(HEAD, HEAD)
            out = jnp.dot(order, block, preferred_element_type=F32).astype(BF16)
            for h in range(heads):
                base = h // count * width + (first + h % count) * HEAD
                o_ref[b * depth:(b + 1) * depth, base:base + HEAD] = out[h * depth:(h + 1) * depth]


def regroup(w_q, w_k, w_v, layer, after):
    depth = w_q.shape[1]
    cols = (w_q.shape[2] + 2 * w_k.shape[2]) * HEAD
    rows = REGROUP_ROWS
    spec = lambda w: pl.BlockSpec((1, rows, w.shape[2], HEAD), lambda i: (layer, i, 0, 0))
    return call(regroup_kernel, (depth // rows,), [spec(w_q), spec(w_k), spec(w_v)],
                pl.BlockSpec((rows, cols), lambda i: (i, 0)), jax.ShapeDtypeStruct((depth, cols), BF16),
                (w_q, w_k, w_v), after=after, cost_estimate=cost(depth * cols * 512, depth * cols * 4))


def norm_rows(x_ref, gain_ref, u_ref, sums_ref, start, rows):
    width = x_ref.shape[1]

    def squares(r):
        at = pl.ds(r, 16)
        total = None
        for cols in tiles(width):
            wide = x_ref[at, cols].astype(F32)
            total = wide * wide if total is None else total + wide * wide
        sums_ref[at, :] = total

    def apply(r):
        at = pl.ds(r, 16)
        inv = sums_ref[at, :]
        for cols in tiles(width):
            u_ref[pl.ds(start + r, 16), cols] = (x_ref[at, cols].astype(F32) * inv * gain_ref[:, cols]).astype(BF16)

    row_blocks(rows, 16, squares)
    to_inv_rms(sums_ref, rows, width)
    row_blocks(rows, 16, apply)


def rope_cols(acc, cos, sin):
    half = HEAD // 2
    a, b = acc[:, :half], acc[:, half:]
    return jnp.concatenate([a * cos - b * sin, b * cos + a * sin], axis=1).astype(BF16)


def qkv0_kernel(x_ref, gain_ref, cos_ref, sin_ref, w_ref, q_ref, kv_ref, u_ref, sums_ref):
    n, m = pl.program_id(0), pl.program_id(1)
    start = pl.multiple_of(m * CHUNK, CHUNK)

    @pl.when(n == 0)
    def _():
        norm_rows(x_ref, gain_ref, u_ref, sums_ref, start, CHUNK)

    acc = jnp.dot(u_ref[pl.ds(start, CHUNK), :], w_ref[...], preferred_element_type=F32)
    cos, sin = cos_ref[...], sin_ref[...]
    per = q_ref.shape[1] // HEAD
    for i in range(per):
        q_ref[:, i * HEAD:(i + 1) * HEAD] = rope_cols(acc[:, i * HEAD:(i + 1) * HEAD], cos, sin)
    kv_ref[:, :HEAD] = rope_cols(acc[:, per * HEAD:(per + 1) * HEAD], cos, sin)
    kv_ref[:, HEAD:] = acc[:, (per + 1) * HEAD:].astype(BF16)


def qkv0(x, gain, cos, sin, w, groups, first, count, after):
    depth, cols = w.shape
    width = cols // groups
    per = width // HEAD - 2
    last = first + count - 1
    hold = lambda n, m: (jnp.where(n == 0, first + m, last), 0)
    rows = lambda n, m: (first + m, 0)
    return call(
        qkv0_kernel, (groups, count),
        [pl.BlockSpec((CHUNK, depth), hold), pl.BlockSpec((1, depth), lambda n, m: (0, 0)),
         pl.BlockSpec((CHUNK, HEAD // 2), rows), pl.BlockSpec((CHUNK, HEAD // 2), rows),
         pl.BlockSpec((depth, width), lambda n, m: (0, n))],
        [pl.BlockSpec((CHUNK, per * HEAD), lambda n, m: (m, n)), pl.BlockSpec((CHUNK, 2 * HEAD), lambda n, m: (m, n))],
        [jax.ShapeDtypeStruct((count * CHUNK, groups * per * HEAD), BF16),
         jax.ShapeDtypeStruct((count * CHUNK, groups * 2 * HEAD), BF16)],
        (x, gain, cos, sin, w), scratch=[pltpu.VMEM((count * CHUNK, depth), BF16), pltpu.VMEM((CHUNK, LANES), F32)], after=after,
        cost_estimate=cost(2 * count * CHUNK * depth * cols, 2 * depth * cols + 4 * count * CHUNK * depth))


def qkv1_kernel(idx_ref, own_ref, peer_ref, gain_ref, cos_ref, sin_ref, w_ref, *rest):
    *out_refs, u_ref, sums_ref = rest
    n = pl.program_id(0)

    @pl.when(n == 0)
    def _():
        t = idx_ref[1]
        norm_rows(own_ref, gain_ref, u_ref, sums_ref, pl.multiple_of(t * HALF, HALF), HALF)
        norm_rows(peer_ref, gain_ref, u_ref, sums_ref, pl.multiple_of((1 - t) * HALF, HALF), HALF)

    acc = jnp.dot(u_ref[...], w_ref[...], preferred_element_type=F32)
    cos, sin = cos_ref[...], sin_ref[...]
    heads = acc.shape[1] // HEAD
    parts = [rope_cols(acc[:, i * HEAD:(i + 1) * HEAD], cos, sin) for i in range(heads - 1)]
    parts.append(acc[:, (heads - 1) * HEAD:].astype(BF16))
    for k, out_ref in enumerate(out_refs):
        @pl.when(n == k)
        def _():
            for i, part in enumerate(parts):
                out_ref[:, i * HEAD:(i + 1) * HEAD] = part


def qkv1(idx, own, peer, gain, cos, sin, w, groups, chunk, after):
    depth, cols = w.shape
    width = cols // groups
    whole = lambda n, idx: (0, 0)
    angle_spec = pl.BlockSpec((CHUNK, HEAD // 2), lambda n, idx: (chunk, 0))
    return call(
        qkv1_kernel, (groups,),
        [pl.BlockSpec((HALF, depth), whole), pl.BlockSpec((HALF, depth), whole), pl.BlockSpec((1, depth), whole),
         angle_spec, angle_spec, pl.BlockSpec((depth, width), lambda n, idx: (0, lax.rem(idx[0] + n, groups)))],
        [pl.BlockSpec((CHUNK, width), whole)] * groups, [jax.ShapeDtypeStruct((CHUNK, width), BF16)] * groups,
        (own, peer, gain, cos, sin, w), scalars=(idx,),
        scratch=[pltpu.VMEM((CHUNK, depth), BF16), pltpu.VMEM((HALF, LANES), F32)], after=after,
        cost_estimate=cost(2 * CHUNK * depth * cols, 2 * depth * cols))


def local_kernel(chunk, idx_ref, q_ref, prev_ref, kv_ref, o_ref):
    lead = jnp.where((idx_ref[0] == 0) & (chunk == 0), CHUNK, 0)
    per = q_ref.shape[1] // HEAD
    scale2 = HEAD ** -0.5 * math.log2(math.e)
    size = CHUNK // 2
    span = WINDOW + size
    for tile in range(CHUNK // size):
        low = tile * size
        q = jnp.concatenate([q_ref[low:low + size, i * HEAD:(i + 1) * HEAD] for i in range(per)], axis=0)
        k = jnp.concatenate([prev_ref[low:, :HEAD], kv_ref[:low + size, :HEAD]], axis=0)
        v = jnp.concatenate([prev_ref[low:, HEAD:], kv_ref[:low + size, HEAD:]], axis=0)
        s = lax.dot_general(q, k, (((1,), (1,)), ((), ())), preferred_element_type=F32)
        row = lax.rem(lax.broadcasted_iota(jnp.int32, (per * size, span), 0), size)
        key = lax.broadcasted_iota(jnp.int32, (per * size, span), 1)
        allowed = (key > row) & (key <= row + WINDOW) & (key >= lead - low)
        s = jnp.where(allowed, s, NEG)
        p = jnp.exp2((s - jnp.max(s, axis=1, keepdims=True)) * scale2)
        weights = (p * (1.0 / jnp.sum(p, axis=1, keepdims=True))).astype(BF16)
        out = jnp.dot(weights, v, preferred_element_type=F32).astype(BF16)
        for i in range(per):
            o_ref[low:low + size, i * HEAD:(i + 1) * HEAD] = out[i * size:(i + 1) * size]


def local_attention(idx, q, prev, kv, groups, chunk, after):
    per = q.shape[1] // groups // HEAD
    block = lambda width: pl.BlockSpec((CHUNK, width * HEAD), lambda g, idx: (0, g))
    return call(
        functools.partial(local_kernel, chunk), (groups,), [block(per), block(2), block(2)],
        block(per), jax.ShapeDtypeStruct((CHUNK, q.shape[1]), BF16), (q, prev, kv), scalars=(idx,), after=after,
        cost_estimate=cost(12 * CHUNK * q.shape[1] * WINDOW, 10 * CHUNK * q.shape[1]))


def global_kernel(chunk, chunks, groups, emit, idx_ref, *refs):
    q_refs, refs = refs[:groups], refs[groups:]
    src_refs, refs = refs[:chunks * groups], refs[chunks * groups:]
    out_refs, refs = refs[:groups], refs[groups:]
    if emit:
        k_out, v_out, *refs = refs
    k_all, v_all, q_all, s_ref, m_ref, l_ref, acc_ref, sems, out_sem = refs
    s = idx_ref[0]
    per = out_refs[0].shape[1] // HEAD
    rows = per * CHUNK
    scale2 = HEAD ** -0.5 * math.log2(math.e)
    lanes = 128
    held = chunks * CHUNK
    source = [lax.rem(s - k + groups, groups) for k in range(groups)]

    copies = []
    for c in range(chunks):
        for k in range(groups):
            at = pl.ds(pl.multiple_of(source[k] * held + c * CHUNK, CHUNK), CHUNK)
            ref = src_refs[c * groups + k]
            for j, dst in ((per, k_all), (per + 1, v_all)):
                copy = pltpu.make_async_copy(ref.at[:, pl.ds(j * HEAD, HEAD)], dst.at[at, :], sems)
                copy.start()
                copies.append(copy)
    for copy in copies:
        copy.wait()
    if emit:
        outs = [pltpu.make_async_copy(k_all, k_out, out_sem.at[0]), pltpu.make_async_copy(v_all, v_out, out_sem.at[1])]
        for copy in outs:
            copy.start()

    def scores(block):
        at = pl.ds(pl.multiple_of(block * CHUNK, CHUNK), CHUNK)
        return lax.dot_general(q_all[...], k_all[at, :], (((1,), (1,)), ((), ())), preferred_element_type=F32)

    def soften(sc, block):
        top = jnp.max(sc, axis=1, keepdims=True)
        before = m_ref[...]
        now = jnp.maximum(before, top)
        m_ref[...] = now
        alpha = jnp.exp2((before - now) * scale2)
        parts = [jnp.exp2((sc[:, i * lanes:(i + 1) * lanes] - now) * scale2) for i in range(CHUNK // lanes)]
        total = parts[0]
        for part in parts[1:]:
            total = total + part
        l_ref[...] = l_ref[...] * alpha + total
        p = jnp.concatenate([part.astype(BF16) for part in parts], axis=1)
        at = pl.ds(pl.multiple_of(block * CHUNK, CHUNK), CHUNK)
        pv = jnp.dot(p, v_all[at, :], preferred_element_type=F32)
        for i in range(HEAD // lanes):
            cols = slice(i * lanes, (i + 1) * lanes)
            acc_ref[:, cols] = acc_ref[:, cols] * alpha + pv[:, cols]

    for k in range(groups):
        for i in range(per):
            q_all[i * CHUNK:(i + 1) * CHUNK, :] = q_refs[k][:, i * HEAD:(i + 1) * HEAD]
        m_ref[...] = jnp.full((rows, lanes), NEG, F32)
        l_ref[...] = jnp.zeros((rows, lanes), F32)
        acc_ref[...] = jnp.zeros((rows, HEAD), F32)
        full = source[k] * chunks + chunk
        s_ref[...] = scores(0)

        def body(block, carry):
            current = s_ref[...]
            following = scores(block + 1)
            soften(current, block)
            s_ref[...] = following
            return carry

        lax.fori_loop(0, full, body, 0)
        row = lax.rem(lax.broadcasted_iota(jnp.int32, (rows, CHUNK), 0), CHUNK)
        key = lax.broadcasted_iota(jnp.int32, (rows, CHUNK), 1)
        soften(jnp.where(key <= row, s_ref[...], NEG), full)
        scale = 1.0 / jnp.sum(l_ref[...], axis=1, keepdims=True)
        out = (acc_ref[...] * scale).astype(BF16)
        for i in range(per):
            out_refs[k][:, i * HEAD:(i + 1) * HEAD] = out[i * CHUNK:(i + 1) * CHUNK]
    if emit:
        for copy in outs:
            copy.wait()


def global_attention(idx, received, chunk, emit, after):
    chunks, groups = len(received), len(received[0])
    per = received[0][0].shape[1] // HEAD - 2
    total = groups * chunks * CHUNK
    rows = per * CHUNK
    any_spec = pl.BlockSpec(memory_space=pl.ANY)
    whole = lambda i, idx: (0, 0)
    out_specs = [pl.BlockSpec((CHUNK, per * HEAD), whole)] * groups
    out_shape = [jax.ShapeDtypeStruct((CHUNK, per * HEAD), BF16)] * groups
    if emit:
        out_specs += [any_spec] * 2
        out_shape += [jax.ShapeDtypeStruct((total, HEAD), BF16)] * 2
    return call(
        functools.partial(global_kernel, chunk, chunks, groups, emit), (1,),
        [pl.BlockSpec((CHUNK, per * HEAD), whole)] * groups + [any_spec] * (chunks * groups), out_specs, out_shape,
        (*received[chunk], *[r for row in received for r in row]), scalars=(idx,),
        scratch=[pltpu.VMEM((total, HEAD), BF16), pltpu.VMEM((total, HEAD), BF16), pltpu.VMEM((rows, HEAD), BF16),
                 pltpu.VMEM((rows, CHUNK), F32), pltpu.VMEM((rows, LANES), F32), pltpu.VMEM((rows, LANES), F32),
                 pltpu.VMEM((rows, HEAD), F32), pltpu.SemaphoreType.DMA(()), pltpu.SemaphoreType.DMA((2,))],
        after=after, cost_estimate=cost(4 * rows * total * HEAD * groups // 2, 4 * total * HEAD))


def o_kernel(groups, split, idx_ref, *refs):
    a_refs, refs = refs[:2 * groups], refs[2 * groups:]
    w_refs, refs = refs[:2 * groups], refs[2 * groups:]
    res_refs, refs = refs[:1 + split], refs[1 + split:]
    gain1_ref, gain2_ref, h_ref, u_ref, acc_ref, sums_ref = refs
    n = pl.program_id(0)

    @pl.when(n == 0)
    def _():
        sums_ref[...] = jnp.zeros(sums_ref.shape, F32)

    total = None
    for a_ref, w_ref in zip(a_refs, w_refs):
        part = jnp.dot(a_ref[...], w_ref[...].reshape(w_ref.shape[-2:]), preferred_element_type=F32)
        total = part if total is None else total + part
    width = total.shape[1]
    acc_ref[:, pl.ds(pl.multiple_of(n * width, LANES), width)] = total
    square = total * total
    sums = sums_ref[...]
    for cols in tiles(width):
        sums = sums + square[:, cols]
    sums_ref[...] = sums

    @pl.when(n == pl.num_programs(0) - 1)
    def _():
        depth = acc_ref.shape[1]
        to_inv_rms(sums_ref, CHUNK, depth)

        def residual(res_ref, start, rows):
            def block(r):
                at = pl.ds(start + r, 16)
                inv = sums_ref[at, :]
                squares = None
                for cols in tiles(depth):
                    mid = (res_ref[pl.ds(r, 16), cols].astype(F32) + acc_ref[at, cols] * inv * gain1_ref[:, cols]).astype(BF16)
                    h_ref[at, cols] = mid
                    wide = mid.astype(F32)
                    squares = wide * wide if squares is None else squares + wide * wide
                sums_ref[at, :] = squares

            row_blocks(rows, 16, block)

        if split:
            t = idx_ref[1]
            residual(res_refs[0], pl.multiple_of(t * HALF, HALF), HALF)
            residual(res_refs[1], pl.multiple_of((1 - t) * HALF, HALF), HALF)
        else:
            residual(res_refs[0], 0, CHUNK)
        to_inv_rms(sums_ref, CHUNK, depth)

        def scale(r):
            at = pl.ds(r, 16)
            inv = sums_ref[at, :]
            for cols in tiles(depth):
                u_ref[at, cols] = (h_ref[at, cols].astype(F32) * inv * gain2_ref[:, cols]).astype(BF16)

        row_blocks(CHUNK, 16, scale)


def o_project(idx, own, peer, w_o, layer, w_peer, residual, chunk, gain1, gain2, after):
    groups = len(w_peer)
    rows, width = w_peer[0].shape
    cols = 768 if width % 768 == 0 else width
    group = lambda k: lambda idx: lax.rem(idx[0] + k, groups)
    a_specs, arrays = [], []
    for a in (own, peer):
        for k in range(groups):
            if isinstance(a, (list, tuple)):
                a_specs.append(pl.BlockSpec((CHUNK, rows), lambda n, idx: (0, 0)))
                arrays.append(a[k])
            else:
                a_specs.append(pl.BlockSpec((CHUNK, rows), lambda n, idx, g=group(k): (0, g(idx))))
                arrays.append(a)
    w_specs = [pl.BlockSpec((1, 1, rows, cols), lambda n, idx, g=group(k): (layer, g(idx), 0, n)) for k in range(groups)]
    w_specs += [pl.BlockSpec((rows, cols), lambda n, idx: (0, n))] * groups
    split = isinstance(residual, (list, tuple))
    if split:
        res_specs, res = [pl.BlockSpec((HALF, width), lambda n, idx: (0, 0))] * 2, list(residual)
    else:
        res_specs, res = [pl.BlockSpec((CHUNK, width), lambda n, idx: (chunk, 0))], [residual]
    gain_spec = pl.BlockSpec((1, width), lambda n, idx: (0, 0))
    out_spec = pl.BlockSpec((CHUNK, width), lambda n, idx: (0, 0))
    return call(
        functools.partial(o_kernel, groups, split), (width // cols,),
        a_specs + w_specs + res_specs + [gain_spec, gain_spec], [out_spec, out_spec],
        [jax.ShapeDtypeStruct((CHUNK, width), BF16)] * 2, (*arrays, *([w_o] * groups), *w_peer, *res, gain1, gain2), scalars=(idx,),
        scratch=[pltpu.VMEM((CHUNK, width), F32), pltpu.VMEM((CHUNK, LANES), F32)], after=after,
        cost_estimate=cost(4 * CHUNK * groups * rows * width, 4 * groups * rows * width))


def mlp_step(u_ref, gate_ref, up_ref, down_ref, acc_ref):
    @pl.when(pl.program_id(0) == 0)
    def _():
        acc_ref[...] = jnp.zeros(acc_ref.shape, F32)

    u = u_ref[...]
    gate = jnp.dot(u, gate_ref[0], preferred_element_type=F32)
    up = jnp.dot(u, up_ref[0], preferred_element_type=F32)
    act = (jax.nn.silu(gate) * up).astype(BF16)
    acc_ref[...] += jnp.dot(act, down_ref[0], preferred_element_type=F32)


def mlp_kernel(idx_ref, u_ref, gate_ref, up_ref, down_ref, own_ref, peer_ref, acc_ref):
    mlp_step(u_ref, gate_ref, up_ref, down_ref, acc_ref)

    @pl.when(pl.program_id(0) == pl.num_programs(0) - 1)
    def _():
        t = idx_ref[1]
        own_ref[...] = acc_ref[pl.ds(pl.multiple_of(t * HALF, HALF), HALF), :]
        peer_ref[...] = acc_ref[pl.ds(pl.multiple_of((1 - t) * HALF, HALF), HALF), :]


def mlp_half_kernel(idx_ref, u_ref, gate_ref, up_ref, down_ref, out_ref):
    mlp_step(u_ref, gate_ref, up_ref, down_ref, out_ref)


def mlp(idx, u, w_gate, w_up, w_down, layer, after, half=None):
    depth, hidden = w_gate.shape[1:]
    block = 512
    whole = lambda n, idx: (0, 0)
    in_spec = pl.BlockSpec((1, depth, block), lambda n, idx: (layer, 0, n))
    w_specs = [in_spec, in_spec, pl.BlockSpec((1, block, depth), lambda n, idx: (layer, n, 0))]
    shape = jax.ShapeDtypeStruct((HALF, depth), F32)
    if half is None:
        return call(mlp_kernel, (hidden // block,), [pl.BlockSpec((CHUNK, depth), whole)] + w_specs,
                    [pl.BlockSpec((HALF, depth), whole)] * 2, [shape] * 2, (u, w_gate, w_up, w_down), scalars=(idx,),
                    scratch=[pltpu.VMEM((CHUNK, depth), F32)], after=after,
                    cost_estimate=cost(6 * CHUNK * depth * hidden, 6 * depth * hidden))
    place = (lambda n, idx: (idx[1], 0)) if half == 'own' else (lambda n, idx: (1 - idx[1], 0))
    return call(mlp_half_kernel, (hidden // block,), [pl.BlockSpec((HALF, depth), place)] + w_specs,
                pl.BlockSpec((HALF, depth), whole), shape, (u, w_gate, w_up, w_down), scalars=(idx,), after=after,
                cost_estimate=cost(6 * HALF * depth * hidden, 6 * depth * hidden))


FINISH_ROWS = 64


def finish_rows(own_ref, got_ref, h_ref, gain_ref, o_ref, sums_ref):
    rows, width = o_ref.shape

    def squares(r):
        at = pl.ds(r, 16)
        total = None
        for cols in tiles(width):
            m = own_ref[at, cols] + got_ref[at, cols]
            total = m * m if total is None else total + m * m
        sums_ref[at, :] = total

    def apply(r):
        at = pl.ds(r, 16)
        inv = sums_ref[at, :]
        for cols in tiles(width):
            m = own_ref[at, cols] + got_ref[at, cols]
            o_ref[at, cols] = (h_ref[at, cols].astype(F32) + m * inv * gain_ref[:, cols]).astype(BF16)

    row_blocks(rows, 16, squares)
    to_inv_rms(sums_ref, rows, width)
    row_blocks(rows, 16, apply)


def finish_kernel(idx_ref, own_ref, got_ref, h_ref, gain_ref, o_ref, sums_ref):
    finish_rows(own_ref, got_ref, h_ref, gain_ref, o_ref, sums_ref)


def finish_place_kernel(idx_ref, own_ref, got_ref, h_ref, gain_ref, *rest):
    o_ref, all_ref, sums_ref = rest[-3:]
    finish_rows(own_ref, got_ref, h_ref, gain_ref, o_ref, sums_ref)
    all_ref[...] = o_ref[...]


def finish(idx, own, got, h, gain, after, place=None):
    width = own.shape[1]
    rows = FINISH_ROWS
    spec = pl.BlockSpec((rows, width), lambda i, idx: (i, 0))
    in_specs = [spec, spec, pl.BlockSpec((rows, width), lambda i, idx: (idx[1] * (HALF // rows) + i, 0)),
                pl.BlockSpec((1, width), lambda i, idx: (0, 0))]
    shape = jax.ShapeDtypeStruct((HALF, width), BF16)
    sums = [pltpu.VMEM((rows, LANES), F32)]
    estimate = cost(HALF * width * 1000, 12 * HALF * width)
    if place is None:
        return call(finish_kernel, (HALF // rows,), in_specs, spec, shape, (own, got, h, gain), scalars=(idx,), scratch=sums,
                    after=after, cost_estimate=estimate)
    out, total, chunk = place
    args, aliases = [own, got, h, gain], {}
    if out is not None:
        args.append(out)
        in_specs.append(pl.BlockSpec(memory_space=pl.ANY))
        aliases = {5: 1}
    at = pl.BlockSpec((rows, width), lambda i, idx: (chunk * (CHUNK // rows) + idx[1] * (HALF // rows) + i, 0))
    return call(finish_place_kernel, (HALF // rows,), in_specs, [spec, at],
                [shape, jax.ShapeDtypeStruct((total, width), BF16)], args, scalars=(idx,), scratch=sums, after=after, aliases=aliases,
                cost_estimate=estimate)


def place_kernel(idx_ref, half_ref, all_ref, out_ref):
    out_ref[...] = half_ref[...]


def place_peer(idx, half, out, chunk, after):
    width = half.shape[1]
    rows = FINISH_ROWS
    at = pl.BlockSpec((rows, width), lambda i, idx: (chunk * (CHUNK // rows) + (1 - idx[1]) * (HALF // rows) + i, 0))
    return call(place_kernel, (HALF // rows,),
                [pl.BlockSpec((rows, width), lambda i, idx: (i, 0)), pl.BlockSpec(memory_space=pl.ANY)], at,
                jax.ShapeDtypeStruct(out.shape, BF16), (half, out), scalars=(idx,), after=after, aliases={2: 0},
                cost_estimate=cost(HALF * width * 300, 4 * HALF * width))


def angles(positions, base):
    half = HEAD // 2
    inv_freq = base ** (-jnp.arange(half, dtype=F32) / half)
    angle = positions.astype(F32)[:, None] * inv_freq
    return jnp.cos(angle), jnp.sin(angle)


def solution(mesh):
    sp = mesh.shape['sp']
    swap = [(0, 1), (1, 0)]

    def shift(value, k):
        return lax.ppermute(value, 'sp', [(i, (i + k) % sp) for i in range(sp)])

    def other(value):
        return lax.ppermute(value, 'tp', swap)

    def device_fn(x, pos, gains, w_q, w_k, w_v, w_o, w_gate, w_up, w_down):
        s, t = lax.axis_index('sp'), lax.axis_index('tp')
        idx = jnp.stack([s, t]).astype(jnp.int32)
        chunks = x.shape[0] // CHUNK
        depth = x.shape[1]
        gain = lambda layer, i: gains[layer, i][None, :]
        w_o4 = w_o.reshape(2, sp, -1, depth)
        rows_o = w_o4.shape[2]
        last = []

        def run(fn, *args, **kw):
            used = [id(v) for v in jax.tree.leaves((args, kw))]
            out = fn(*args, after=tuple(v for v in last if id(v) not in used), **kw)
            last[:] = [out[0] if isinstance(out, (list, tuple)) else out]
            return out

        def gather_w_o(layer):
            mine = lax.dynamic_slice(w_o4, (layer, s, 0, 0), (1, 1, rows_o, depth)).reshape(rows_o, depth)
            got = other(mine)
            return [got] + [shift(got, -k) for k in range(1, sp)]

        def mlp_phase(layer, steps, tail, place):
            mids, sums, got, mine, theirs = [], [], [], [], []
            out = None

            def close(c):
                nonlocal out
                own = run(finish, idx, sums[c], got[c], mids[c][0], gain(layer, 3),
                          place=(out, x.shape[0], c) if place else None)
                if place:
                    own, out = own
                mine.append(own)
                theirs.append(other(own))

            def put(c):
                nonlocal out
                out = run(place_peer, idx, theirs[c], out, c)

            def late(c):
                tail(c, mine, theirs) if tail else put(c)

            end = chunks - 1
            for c in range(chunks):
                mids.append(run(o_project, *steps(c)))
                if c == end and c > 0:
                    close(c - 1)
                mlp_of = lambda **kw: run(mlp, idx, mids[c][1], w_gate, w_up, w_down, layer, **kw)
                if c in (0, end):
                    got.append(other(mlp_of(half='peer')))
                    sums.append(mlp_of(half='own'))
                else:
                    own, peer = mlp_of()
                    sums.append(own)
                    got.append(other(peer))
                    close(c - 1)
                if 2 <= c:
                    late(c - 2)
            close(end)
            late(end - 1)
            late(end)
            return mine, theirs, out

        end = chunks - 1
        w_peer0 = gather_w_o(0)
        wide0 = run(regroup, w_q, w_k, w_v, 0)
        cos0, sin0 = angles(pos, LOCAL_BASE)
        project = lambda c: run(qkv0, x, gain(0, 0), cos0, sin0, wide0, sp, c, 1)
        q_tail, kv_tail = project(end)
        prev = shift(kv_tail, 1)

        tails = [kv_tail[:, g * 2 * HEAD:(g + 1) * 2 * HEAD] for g in range(sp)]
        local_kv = jnp.where(s == sp - 1, tails[sp - 1], jnp.zeros_like(tails[0]))
        for g in range(sp - 1):
            local_kv = local_kv + lax.ppermute(tails[g], 'sp', [(sp - 1, g)])

        attn, attn_peer = [], []
        for c in range(chunks):
            q, kv = project(c) if c < end else (q_tail, kv_tail)
            attn.append(run(local_attention, idx, q, prev, kv, sp, c))
            attn_peer.append(other(attn[c]))
            prev = kv
        wide1 = run(regroup, w_q, w_k, w_v, 1)
        cos1, sin1 = angles(lax.optimization_barrier((pos, attn[end]))[0], GLOBAL_BASE)
        w_peer1 = gather_w_o(1)
        received = []

        def to_heads(c, mine, theirs):
            blocks = run(qkv1, idx, mine[c], theirs[c], gain(1, 0), cos1, sin1, wide1, sp, c)
            received.append([blocks[0]] + [shift(blocks[k], k) for k in range(1, sp)])

        mine, theirs, _ = mlp_phase(
            0, lambda c: (idx, attn[c], attn_peer[c], w_o4, 0, w_peer0, x, c, gain(0, 1), gain(0, 2)), to_heads, False)

        owns, peers = [], []
        for c in range(chunks):
            outs = run(global_attention, idx, received, c, c == 0)
            if c == 0:
                k_global, v_global = outs[sp:]
            owns.append([outs[0]] + [shift(outs[k], -k) for k in range(1, sp)])
            peers.append([other(a) for a in owns[c]])
        _, _, out = mlp_phase(
            1, lambda c: (idx, owns[c], peers[c], w_o4, 1, w_peer1, (mine[c], theirs[c]), c, gain(1, 1), gain(1, 2)), None, True)
        cache = lambda value: value[:, None, :]
        return out, cache(local_kv[:, :HEAD]), cache(local_kv[:, HEAD:]), cache(k_global), cache(v_global)

    token_spec = P(('rep', 'sp'), None)
    cache_spec = P('rep', ('tp', 'sp'), None)
    in_specs = (token_spec, P(('rep', 'sp')), P(), P(None, None, 'tp', None), P(None, None, 'tp', None),
                P(None, None, 'tp', None), P(None, 'tp', None, None), P(None, None, 'tp'), P(None, None, 'tp'),
                P(None, 'tp', None))
    out_specs = (token_spec, cache_spec, cache_spec, cache_spec, cache_spec)

    step = jax.shard_map(device_fn, mesh=mesh, in_specs=in_specs, out_specs=out_specs, check_vma=False)

    def program(*args):
        jax.eval_shape(step, *args)
        return step(*args)

    return program
```

time: 6030 us -> 2540 us (0.42)
  waiting for transfers between devices: 3080 us -> 637 us
  matrix products: 1860 us -> 0 us
  Pallas kernels: 0 us -> 1770 us
  other arithmetic: 497 us -> 13.8 us
  local copies, waits for them, and re-layouts: 314 us -> 12.6 us
  blocking collectives: 194 us -> 0 us
  starting transfers between devices: 14.1 us -> 95.1 us
    psum x4 -> x0, waiting for transfers between devices: 2710 us -> none  [the longest x2 1370 us: layer(): lax.psum(jnp.einsum('the,hed->td', attn_back, w_o, preferred_element_type...]
    dot_general x142 -> x0, matrix products: 1860 us -> none  [the longest x64 417 us: one_block(): jnp.einsum('qhgd,khd->hgqk', q_tile, k_tile, preferred_element_type=jnp.f...]
    pallas_call x0 -> x50, Pallas kernels: none -> 1770 us  [call(): pl.pallas_call(wrapped, grid_spec=pltpu.PrefetchScalarGridSpec(num_scalar...]
    ppermute x0 -> x72, waiting for transfers between devices: none -> 637 us  [the longest x38 382 us: other(): return lax.ppermute(value, 'tp', swap)]
    reduce_sum x72 -> x0, other arithmetic: 378 us -> none  [the longest x64 272 us: one_block(): jax.nn.softmax(jnp.where(allowed, scores, -1e+30), axis=-1)]
    all_to_all x2 -> x0, waiting for transfers between devices: 366 us -> none  [layer(): received = lax.all_to_all(outgoing, 'sp', 1, 0, tiled=True)]
    all_to_all x2 -> x0, blocking collectives: 194 us -> none  [layer(): lax.all_to_all(attn_out, 'sp', 0, 2, tiled=True)]
    ppermute x0 -> x72, starting transfers between devices: none -> 95.1 us  [the longest x31 53.3 us: shift(): return lax.ppermute(value, 'sp', [(i, (i + k) % sp) for i in range(sp)])]
  transfers between devices with their start and end apart: 6 -> 72, of which waited for: 6 -> 27; matrix products, arithmetic and copies ran while one was open for 1% -> 1% of each run, Pallas kernels for 0% -> 67%
where the time goes in v1:
time: 2540 us; the launch traced here: 2530 us
  Pallas kernels  1770 us (70%)
  waiting for transfers between devices  637 us (25%)
  starting transfers between devices  95.1 us (4%)
    pallas_call x50, Pallas kernels, call(): pl.pallas_call(wrapped, grid_spec=pltpu.PrefetchScalarGridSpec(num_scalar...  1770 us
    ppermute x38, waiting for transfers between devices, other(): return lax.ppermute(value, 'tp', swap)  382 us
    ppermute x31, waiting for transfers between devices, shift(): return lax.ppermute(value, 'sp', [(i, (i + k) % sp) for i in range(sp)])  249 us
    ppermute x31, starting transfers between devices, shift(): return lax.ppermute(value, 'sp', [(i, (i + k) % sp) for i in range(sp)])  53.3 us
  transfers between devices with their start and end apart: 72, of which 27 were waited for; matrix products, arithmetic and copies ran while one was open for 1% of the time, Pallas kernels for 67%

profile of v1, /device:TPU:0, one launch (start us, length us, event | category | flops | bytes accessed | tf_op | source)
XLA Modules:
  0.0 2525.5 jit_solution(10219277922634114737)
XLA Ops:
  8.8 36.6 %shard_map.137.refs_4_ = bf16[3840,4096]{1,0:T(8,128)(2,1)} custom-call(bf16[2,3840,8,256]{3,2,1,0:T(8,128)(2,1)} %refs_0_.11, bf16[2,3840,4,256]{3,2,1,0:T(4,128)(2,1)} %refs_1_.3, bf16[2,3840,4,256]{3,2,1,0:T(4,128)(2,1)} %refs_2_.15), custom_call_target="tpu_custom_call" | custom-call | flops 8053063680 | bytes 62914560 | tf_op jit(solution)/shard_map/pallas_call | solution.py:33
  227.1 36.6 %shard_map.146.refs_20_.refs_6_ = bf16[3840,4096]{1,0:T(8,128)(2,1)} custom-call(bf16[2,3840,8,256]{3,2,1,0:T(8,128)(2,1)} %refs_0_.11, bf16[2,3840,4,256]{3,2,1,0:T(4,128)(2,1)} %refs_1_.3, bf16[2,3840,4,256]{3,2,1,0:T(4,128)(2,1)} %refs_2_.15, bf16[512,2048]{1,0:T(8,128)(2,1)} %shard_map.145.refs_3_.refs_1_.refs_2_.refs_4_), custom_call_target="tpu_custom_call" | custom-call | flops 8053063680 | bytes 62914560 | tf_op jit(solution)/shard_map/pallas_call | solution.py:33
  264.2 75.4 %collective-permute-done.4.refs_15_ = bf16[512,3840]{1,0:T(8,128)(2,1)} collective-permute-done((bf16[512,3840]{1,0:T(8,128)(2,1)}, bf16[512,3840]{1,0:T(8,128)(2,1)}, u32[]{:S(2)}, u32[]{:S(2)}) %collective-permute-start.4) | collective-permute-done | bytes 3932192 | tf_op jit(solution)/shard_map/ppermute | solution.py:556
  370.7 68.0 %shard_map.148.refs_5_ = f32[256,3840]{1,0:T(8,128)} custom-call(s32[2]{0:T(128)} %pad_add_fusion.refs_0_, bf16[512,3840]{1,0:T(8,128)(2,1)} %get-tuple-element.88.refs_1_, bf16[2,3840,7680]{2,1,0:T(8,128)(2,1)} %refs_2_.27, bf16[2,3840,7680]{2,1,0:T(8,128)(2,1)} %refs_3_.23, bf16[2,7680,3840]{2,1,0:T(8,128)(2,1)} %refs_4_.23, ...), custom_call_target="tpu_custom_call" | custom-call | flops 45298483200 | bytes 176947200 | tf_op jit(solution)/shard_map/pallas_call | solution.py:33
  438.7 67.5 %shard_map.149.refs_20_.refs_1_ = f32[256,3840]{1,0:T(8,128)} custom-call(s32[2]{0:T(128)} %pad_add_fusion.refs_0_, bf16[512,3840]{1,0:T(8,128)(2,1)} %get-tuple-element.88.refs_1_, bf16[2,3840,7680]{2,1,0:T(8,128)(2,1)} %refs_2_.27, bf16[2,3840,7680]{2,1,0:T(8,128)(2,1)} %refs_3_.23, bf16[2,7680,3840]{2,1,0:T(8,128)(2,1)} %refs_4_.23, ...), custom_call_target="tpu_custom_call" | custom-call | flops 45298483200 | bytes 176947200 | tf_op jit(solution)/shard_map/pallas_call | solution.py:33
  538.9 108.3 %shard_map.151 = (f32[256,3840]{1,0:T(8,128)}, f32[256,3840]{1,0:T(8,128)}) custom-call(s32[2]{0:T(128)} %pad_add_fusion.refs_0_, bf16[512,3840]{1,0:T(8,128)(2,1)} %get-tuple-element.90.refs_1_, bf16[2,3840,7680]{2,1,0:T(8,128)(2,1)} %refs_2_.27, bf16[2,3840,7680]{2,1,0:T(8,128)(2,1)} %refs_3_.23, bf16[2,7680,3840]{2,1,0:T(8,128)(2,1)} %refs_4_.23, ...), custom_call_target="tpu_custom_call" | custom-call | flops 90596966400 | bytes 176947200 | tf_op jit(solution)/shard_map/pallas_call | solution.py:33
  687.4 108.4 %shard_map.154 = (f32[256,3840]{1,0:T(8,128)}, f32[256,3840]{1,0:T(8,128)}) custom-call(s32[2]{0:T(128)} %pad_add_fusion.refs_0_, bf16[512,3840]{1,0:T(8,128)(2,1)} %get-tuple-element.95.refs_1_, bf16[2,3840,7680]{2,1,0:T(8,128)(2,1)} %refs_2_.27, bf16[2,3840,7680]{2,1,0:T(8,128)(2,1)} %refs_3_.23, bf16[2,7680,3840]{2,1,0:T(8,128)(2,1)} %refs_4_.23, ...), custom_call_target="tpu_custom_call" | custom-call | flops 90596966400 | bytes 176947200 | tf_op jit(solution)/shard_map/pallas_call | solution.py:33
  839.9 173.3 %collective-permute-done.1.refs_5_.refs_6_.refs_7_.refs_8_ = bf16[512,2048]{1,0:T(8,128)(2,1)} collective-permute-done((bf16[512,2048]{1,0:T(8,128)(2,1)}, bf16[512,2048]{1,0:T(8,128)(2,1)}, u32[]{:S(2)}, u32[]{:S(2)}) %collective-permute-start.1) | collective-permute-done | bytes 2097184 | tf_op jit(solution)/shard_map/ppermute | solution.py:559
  1013.2 31.5 %shard_map.157 = (bf16[512,3840]{1,0:T(8,128)(2,1)}, bf16[512,3840]{1,0:T(8,128)(2,1)}) custom-call(s32[2]{0:T(128)} %pad_add_fusion.refs_0_, bf16[512,2048]{1,0:T(8,128)(2,1)} %shard_map.145.refs_3_.refs_1_.refs_2_.refs_4_, bf16[512,2048]{1,0:T(8,128)(2,1)} %shard_map.145.refs_3_.refs_1_.refs_2_.refs_4_, ...), custom_call_target="tpu_custom_call" | custom-call | flops 16106127360 | bytes 31457280 | tf_op jit(solution)/shard_map/pallas_call | solution.py:33
  1051.7 67.5 %shard_map.159.refs_5_ = f32[256,3840]{1,0:T(8,128)} custom-call(s32[2]{0:T(128)} %pad_add_fusion.refs_0_, bf16[512,3840]{1,0:T(8,128)(2,1)} %get-tuple-element.99.refs_1_, bf16[2,3840,7680]{2,1,0:T(8,128)(2,1)} %refs_2_.27, bf16[2,3840,7680]{2,1,0:T(8,128)(2,1)} %refs_3_.23, bf16[2,7680,3840]{2,1,0:T(8,128)(2,1)} %refs_4_.23, ...), custom_call_target="tpu_custom_call" | custom-call | flops 45298483200 | bytes 176947200 | tf_op jit(solution)/shard_map/pallas_call | solution.py:33
  1119.8 67.6 %shard_map.160.refs_7_.refs_1_ = f32[256,3840]{1,0:T(8,128)} custom-call(s32[2]{0:T(128)} %pad_add_fusion.refs_0_, bf16[512,3840]{1,0:T(8,128)(2,1)} %get-tuple-element.99.refs_1_, bf16[2,3840,7680]{2,1,0:T(8,128)(2,1)} %refs_2_.27, bf16[2,3840,7680]{2,1,0:T(8,128)(2,1)} %refs_3_.23, bf16[2,7680,3840]{2,1,0:T(8,128)(2,1)} %refs_4_.23, ...), custom_call_target="tpu_custom_call" | custom-call | flops 45298483200 | bytes 176947200 | tf_op jit(solution)/shard_map/pallas_call | solution.py:33
  1414.6 31.4 %shard_map.165 = (bf16[512,512]{1,0:T(8,128)(2,1)}, bf16[512,512]{1,0:T(8,128)(2,1)}, bf16[512,512]{1,0:T(8,128)(2,1)}, bf16[512,512]{1,0:T(8,128)(2,1)}, bf16[8...) custom-call(s32[2]{0:T(128)} %pad_add_fusion.refs_0_, bf16[512,1024]{1,0:T(8,128)(2,1)} %get-tuple-element.98.refs_20_.refs_1_.refs_5_, ...), custom_call_target="tpu_custom_call" | custom-call | flops 17179869184 | bytes 8388608 | tf_op jit(solution)/shard_map/pallas_call | solution.py:33
  1449.2 33.9 %shard_map.166 = (bf16[512,512]{1,0:T(8,128)(2,1)}, bf16[512,512]{1,0:T(8,128)(2,1)}, bf16[512,512]{1,0:T(8,128)(2,1)}, bf16[512,512]{1,0:T(8,128)(2,1)}) custom-call(s32[2]{0:T(128)} %pad_add_fusion.refs_0_, bf16[512,1024]{1,0:T(8,128)(2,1)} %get-tuple-element.102.refs_5_.refs_9_.refs_1_, bf16[512,1024]{1,0:T(8,128)(2,1)} %collective-permute-done.23.refs_10_.refs_2_, ...), custom_call_target="tpu_custom_call" | custom-call | flops 17179869184 | bytes 8388608 | tf_op jit(solution)/shard_map/pallas_call | solution.py:33
  1500.7 37.4 %shard_map.167 = (bf16[512,512]{1,0:T(8,128)(2,1)}, bf16[512,512]{1,0:T(8,128)(2,1)}, bf16[512,512]{1,0:T(8,128)(2,1)}, bf16[512,512]{1,0:T(8,128)(2,1)}) custom-call(s32[2]{0:T(128)} %pad_add_fusion.refs_0_, bf16[512,1024]{1,0:T(8,128)(2,1)} %get-tuple-element.103.refs_7_.refs_13_.refs_1_, bf16[512,1024]{1,0:T(8,128)(2,1)} %collective-permute-done.26.refs_14_.refs_2_, ...), custom_call_target="tpu_custom_call" | custom-call | flops 17179869184 | bytes 8388608 | tf_op jit(solution)/shard_map/pallas_call | solution.py:33
  1538.0 46.8 %collective-permute-done.38.refs_15_ = bf16[512,3840]{1,0:T(8,128)(2,1)} collective-permute-done((bf16[512,3840]{1,0:T(8,128)(2,1)}, bf16[512,3840]{1,0:T(8,128)(2,1)}, u32[]{:S(2)}, u32[]{:S(2)}) %collective-permute-start.38) | collective-permute-done | bytes 3932192 | tf_op jit(solution)/shard_map/ppermute | solution.py:556
  1608.2 40.5 %shard_map.168 = (bf16[512,512]{1,0:T(8,128)(2,1)}, bf16[512,512]{1,0:T(8,128)(2,1)}, bf16[512,512]{1,0:T(8,128)(2,1)}, bf16[512,512]{1,0:T(8,128)(2,1)}) custom-call(s32[2]{0:T(128)} %pad_add_fusion.refs_0_, bf16[512,1024]{1,0:T(8,128)(2,1)} %get-tuple-element.104.refs_17_.refs_1_, bf16[512,1024]{1,0:T(8,128)(2,1)} %collective-permute-done.17.refs_18_.refs_2_, ...), custom_call_target="tpu_custom_call" | custom-call | flops 17179869184 | bytes 8388608 | tf_op jit(solution)/shard_map/pallas_call | solution.py:33
  1682.7 67.4 %shard_map.170.refs_5_ = f32[256,3840]{1,0:T(8,128)} custom-call(s32[2]{0:T(128)} %pad_add_fusion.refs_0_, bf16[512,3840]{1,0:T(8,128)(2,1)} %get-tuple-element.127.refs_1_, bf16[2,3840,7680]{2,1,0:T(8,128)(2,1)} %refs_2_.27, bf16[2,3840,7680]{2,1,0:T(8,128)(2,1)} %refs_3_.23, bf16[2,7680,3840]{2,1,0:T(8,128)(2,1)} %refs_4_.23, ...), custom_call_target="tpu_custom_call" | custom-call | flops 45298483200 | bytes 176947200 | tf_op jit(solution)/shard_map/pallas_call | solution.py:33
  1755.4 67.3 %shard_map.171.refs_21_.refs_1_ = f32[256,3840]{1,0:T(8,128)} custom-call(s32[2]{0:T(128)} %pad_add_fusion.refs_0_, bf16[512,3840]{1,0:T(8,128)(2,1)} %get-tuple-element.127.refs_1_, bf16[2,3840,7680]{2,1,0:T(8,128)(2,1)} %refs_2_.27, bf16[2,3840,7680]{2,1,0:T(8,128)(2,1)} %refs_3_.23, bf16[2,7680,3840]{2,1,0:T(8,128)(2,1)} %refs_4_.23, ...), custom_call_target="tpu_custom_call" | custom-call | flops 45298483200 | bytes 176947200 | tf_op jit(solution)/shard_map/pallas_call | solution.py:33
  1858.2 108.1 %shard_map.173 = (f32[256,3840]{1,0:T(8,128)}, f32[256,3840]{1,0:T(8,128)}) custom-call(s32[2]{0:T(128)} %pad_add_fusion.refs_0_, bf16[512,3840]{1,0:T(8,128)(2,1)} %get-tuple-element.132.refs_1_, bf16[2,3840,7680]{2,1,0:T(8,128)(2,1)} %refs_2_.27, bf16[2,3840,7680]{2,1,0:T(8,128)(2,1)} %refs_3_.23, bf16[2,7680,3840]{2,1,0:T(8,128)(2,1)} %refs_4_.23, ...), custom_call_target="tpu_custom_call" | custom-call | flops 90596966400 | bytes 176947200 | tf_op jit(solution)/shard_map/pallas_call | solution.py:33
  2007.2 108.3 %shard_map.176 = (f32[256,3840]{1,0:T(8,128)}, f32[256,3840]{1,0:T(8,128)}) custom-call(s32[2]{0:T(128)} %pad_add_fusion.refs_0_, bf16[512,3840]{1,0:T(8,128)(2,1)} %get-tuple-element.141.refs_1_, bf16[2,3840,7680]{2,1,0:T(8,128)(2,1)} %refs_2_.27, bf16[2,3840,7680]{2,1,0:T(8,128)(2,1)} %refs_3_.23, bf16[2,7680,3840]{2,1,0:T(8,128)(2,1)} %refs_4_.23, ...), custom_call_target="tpu_custom_call" | custom-call | flops 90596966400 | bytes 176947200 | tf_op jit(solution)/shard_map/pallas_call | solution.py:33
  2156.6 58.3 %collective-permute-done.32.refs_5_ = bf16[512,512]{1,0:T(8,128)(2,1)} collective-permute-done((bf16[512,512]{1,0:T(8,128)(2,1)S(1)}, bf16[512,512]{1,0:T(8,128)(2,1)}, u32[]{:S(2)}, u32[]{:S(2)}) %collective-permute-start.32) | collective-permute-done | bytes 524320 | tf_op jit(solution)/shard_map/ppermute | solution.py:559
  2286.8 67.7 %shard_map.181.refs_5_ = f32[256,3840]{1,0:T(8,128)} custom-call(s32[2]{0:T(128)} %pad_add_fusion.refs_0_, bf16[512,3840]{1,0:T(8,128)(2,1)} %get-tuple-element.146.refs_1_, bf16[2,3840,7680]{2,1,0:T(8,128)(2,1)} %refs_2_.27, bf16[2,3840,7680]{2,1,0:T(8,128)(2,1)} %refs_3_.23, bf16[2,7680,3840]{2,1,0:T(8,128)(2,1)} %refs_4_.23, ...), custom_call_target="tpu_custom_call" | custom-call | flops 45298483200 | bytes 176947200 | tf_op jit(solution)/shard_map/pallas_call | solution.py:33
  2355.7 67.4 %shard_map.182.refs_3_.refs_1_ = f32[256,3840]{1,0:T(8,128)} custom-call(s32[2]{0:T(128)} %pad_add_fusion.refs_0_, bf16[512,3840]{1,0:T(8,128)(2,1)} %get-tuple-element.146.refs_1_, bf16[2,3840,7680]{2,1,0:T(8,128)(2,1)} %refs_2_.27, bf16[2,3840,7680]{2,1,0:T(8,128)(2,1)} %refs_3_.23, bf16[2,7680,3840]{2,1,0:T(8,128)(2,1)} %refs_4_.23, ...), custom_call_target="tpu_custom_call" | custom-call | flops 45298483200 | bytes 176947200 | tf_op jit(solution)/shard_map/pallas_call | solution.py:33
  2489.1 31.6 %collective-permute-done.67.refs_1_ = bf16[256,3840]{1,0:T(8,128)(2,1)} collective-permute-done((bf16[256,3840]{1,0:T(8,128)(2,1)}, bf16[256,3840]{1,0:T(8,128)(2,1)}, u32[]{:S(2)}, u32[]{:S(2)}) %collective-permute-start.67) | collective-permute-done | bytes 1966112 | tf_op jit(solution)/shard_map/ppermute | solution.py:559
  (214 shorter events, 917.3 us)
Async XLA Ops:
  116.8 146.9 %collective-permute-start.6 = (bf16[512,2048]{1,0:T(8,128)(2,1)}, bf16[512,2048]{1,0:T(8,128)(2,1)}, u32[]{:S(2)}, u32[]{:S(2)}) collective-permute-start(bf16[512,2048]{1,0:T(8,128)(2,1)} %shard_map.140.refs_5_.refs_1_.refs_2_.refs_3_.refs_4_), channel_id=1, source_target_pairs={{0,4},{4,0},{1,5},{5,1},{2,6},{6,2},{3,7},{7,3}} | collective-permute-start | bytes 6291464 | tf_op jit(solution)/shard_map/ppermute | solution.py:559
  167.5 172.1 %collective-permute-start.4 = (bf16[512,3840]{1,0:T(8,128)(2,1)}, bf16[512,3840]{1,0:T(8,128)(2,1)}, u32[]{:S(2)}, u32[]{:S(2)}) collective-permute-start(bf16[512,3840]{1,0:T(8,128)(2,1)} %collective-permute-done.2.refs_13_), channel_id=1, source_target_pairs={{0,2},{1,3},{2,0},{3,1},{4,6},{5,7},{6,4},{7,5}} | collective-permute-start | bytes 11796488 | tf_op jit(solution)/shard_map/ppermute | solution.py:556
  169.8 169.8 %collective-permute-start.5 = (bf16[512,3840]{1,0:T(8,128)(2,1)}, bf16[512,3840]{1,0:T(8,128)(2,1)}, u32[]{:S(2)}, u32[]{:S(2)}) collective-permute-start(bf16[512,3840]{1,0:T(8,128)(2,1)} %collective-permute-done.2.refs_13_), channel_id=1, source_target_pairs={{0,1},{1,2},{2,3},{3,0},{4,5},{5,6},{6,7},{7,4}} | collective-permute-start | bytes 11796488 | tf_op jit(solution)/shard_map/ppermute | solution.py:556
  205.2 302.6 %collective-permute-start.8 = (bf16[512,2048]{1,0:T(8,128)(2,1)}, bf16[512,2048]{1,0:T(8,128)(2,1)}, u32[]{:S(2)}, u32[]{:S(2)}) collective-permute-start(bf16[512,2048]{1,0:T(8,128)(2,1)} %shard_map.142.refs_5_.refs_1_.refs_2_.refs_3_.refs_4_), channel_id=1, source_target_pairs={{0,4},{4,0},{1,5},{5,1},{2,6},{6,2},{3,7},{7,3}} | collective-permute-start | bytes 6291464 | tf_op jit(solution)/shard_map/ppermute | solution.py:559
  263.7 392.6 %collective-permute-start.11 = (bf16[512,2048]{1,0:T(8,128)(2,1)}, bf16[512,2048]{1,0:T(8,128)(2,1)}, u32[]{:S(2)}, u32[]{:S(2)}) collective-permute-start(bf16[512,2048]{1,0:T(8,128)(2,1)} %shard_map.144.refs_4_.refs_1_.refs_2_.refs_3_), channel_id=1, source_target_pairs={{0,4},{4,0},{1,5},{5,1},{2,6},{6,2},{3,7},{7,3}} | collective-permute-start | bytes 6291464 | tf_op jit(solution)/shard_map/ppermute | solution.py:559
  647.2 156.7 %collective-permute-start.10 = (f32[256,3840]{1,0:T(8,128)}, f32[256,3840]{1,0:T(8,128)}, u32[]{:S(2)}, u32[]{:S(2)}) collective-permute-start(f32[256,3840]{1,0:T(8,128)} %get-tuple-element.94), channel_id=1, source_target_pairs={{0,4},{4,0},{1,5},{5,1},{2,6},{6,2},{3,7},{7,3}} | collective-permute-start | bytes 11796488 | tf_op jit(solution)/shard_map/ppermute | solution.py:559
  654.8 157.7 %collective-permute-start.9 = (bf16[256,3840]{1,0:T(8,128)(2,1)}, bf16[256,3840]{1,0:T(8,128)(2,1)}, u32[]{:S(2)}, u32[]{:S(2)}) collective-permute-start(bf16[256,3840]{1,0:T(8,128)(2,1)} %shard_map.152.refs_20_.refs_1_.refs_17_), channel_id=1, source_target_pairs={{0,4},{4,0},{1,5},{5,1},{2,6},{6,2},{3,7},{7,3}} | collective-permute-start | bytes 5898248 | tf_op jit(solution)/shard_map/ppermute | solution.py:559
  795.8 248.9 %collective-permute-start.12 = (f32[256,3840]{1,0:T(8,128)}, f32[256,3840]{1,0:T(8,128)}, u32[]{:S(2)}, u32[]{:S(2)}) collective-permute-start(f32[256,3840]{1,0:T(8,128)} %get-tuple-element.100), channel_id=1, source_target_pairs={{0,4},{4,0},{1,5},{5,1},{2,6},{6,2},{3,7},{7,3}} | collective-permute-start | bytes 11796488 | tf_op jit(solution)/shard_map/ppermute | solution.py:559
  796.3 480.7 %collective-permute-start.36 = (bf16[512,3840]{1,0:T(8,128)(2,1)}, bf16[512,3840]{1,0:T(8,128)(2,1)}, u32[]{:S(2)}, u32[]{:S(2)}) collective-permute-start(bf16[512,3840]{1,0:T(8,128)(2,1)} %get-tuple-element.155), channel_id=1, source_target_pairs={{0,4},{4,0},{1,5},{5,1},{2,6},{6,2},{3,7},{7,3}} | collective-permute-start | bytes 11796488 | tf_op jit(solution)/shard_map/ppermute | solution.py:559
  797.8 215.3 %collective-permute-start.1 = (bf16[512,2048]{1,0:T(8,128)(2,1)}, bf16[512,2048]{1,0:T(8,128)(2,1)}, u32[]{:S(2)}, u32[]{:S(2)}) collective-permute-start(bf16[512,2048]{1,0:T(8,128)(2,1)} %shard_map.145.refs_3_.refs_1_.refs_2_.refs_4_), channel_id=1, source_target_pairs={{0,4},{4,0},{1,5},{5,1},{2,6},{6,2},{3,7},{7,3}} | collective-permute-start | bytes 6291464 | tf_op jit(solution)/shard_map/ppermute | solution.py:559
  810.9 377.9 %collective-permute-start.14 = (bf16[256,3840]{1,0:T(8,128)(2,1)}, bf16[256,3840]{1,0:T(8,128)(2,1)}, u32[]{:S(2)}, u32[]{:S(2)}) collective-permute-start(bf16[256,3840]{1,0:T(8,128)(2,1)} %shard_map.155.refs_7_.refs_1_.refs_17_), channel_id=1, source_target_pairs={{0,4},{4,0},{1,5},{5,1},{2,6},{6,2},{3,7},{7,3}} | collective-permute-start | bytes 5898248 | tf_op jit(solution)/shard_map/ppermute | solution.py:559
  1348.9 150.0 %collective-permute-start.37 = (bf16[512,3840]{1,0:T(8,128)(2,1)}, bf16[512,3840]{1,0:T(8,128)(2,1)}, u32[]{:S(2)}, u32[]{:S(2)}) collective-permute-start(bf16[512,3840]{1,0:T(8,128)(2,1)} %collective-permute-done.36.refs_13_), channel_id=1, source_target_pairs={{0,3},{1,0},{2,1},{3,2},{4,7},{5,4},{6,5},{7,6}} | collective-permute-start | bytes 11796488 | tf_op jit(solution)/shard_map/ppermute | solution.py:556
  1369.6 215.2 %collective-permute-start.38 = (bf16[512,3840]{1,0:T(8,128)(2,1)}, bf16[512,3840]{1,0:T(8,128)(2,1)}, u32[]{:S(2)}, u32[]{:S(2)}) collective-permute-start(bf16[512,3840]{1,0:T(8,128)(2,1)} %collective-permute-done.36.refs_13_), channel_id=1, source_target_pairs={{0,2},{1,3},{2,0},{3,1},{4,6},{5,7},{6,4},{7,5}} | collective-permute-start | bytes 11796488 | tf_op jit(solution)/shard_map/ppermute | solution.py:556
  1391.6 257.1 %collective-permute-start.39 = (bf16[512,3840]{1,0:T(8,128)(2,1)}, bf16[512,3840]{1,0:T(8,128)(2,1)}, u32[]{:S(2)}, u32[]{:S(2)}) collective-permute-start(bf16[512,3840]{1,0:T(8,128)(2,1)} %collective-permute-done.36.refs_13_), channel_id=1, source_target_pairs={{0,1},{1,2},{2,3},{3,0},{4,5},{5,6},{6,7},{7,4}} | collective-permute-start | bytes 11796488 | tf_op jit(solution)/shard_map/ppermute | solution.py:556
  1446.0 148.3 %collective-permute-start.40 = (bf16[512,512]{1,0:T(8,128)(2,1)}, bf16[512,512]{1,0:T(8,128)(2,1)S(1)}, u32[]{:S(2)}, u32[]{:S(2)}) collective-permute-start(bf16[512,512]{1,0:T(8,128)(2,1)} %get-tuple-element.124), channel_id=1, source_target_pairs={{0,3},{1,0},{2,1},{3,2},{4,7},{5,4},{6,5},{7,6}} | collective-permute-start | bytes 1572872 | tf_op jit(solution)/shard_map/ppermute | solution.py:556
  1447.9 158.3 %collective-permute-start.41 = (bf16[512,512]{1,0:T(8,128)(2,1)}, bf16[512,512]{1,0:T(8,128)(2,1)}, u32[]{:S(2)}, u32[]{:S(2)}) collective-permute-start(bf16[512,512]{1,0:T(8,128)(2,1)} %get-tuple-element.125), channel_id=1, source_target_pairs={{0,2},{1,3},{2,0},{3,1},{4,6},{5,7},{6,4},{7,5}} | collective-permute-start | bytes 1572872 | tf_op jit(solution)/shard_map/ppermute | solution.py:556
  1822.7 152.9 %collective-permute-start.60 = (bf16[512,512]{1,0:T(8,128)(2,1)S(1)}, bf16[512,512]{1,0:T(8,128)(2,1)S(1)}, u32[]{:S(2)}, u32[]{:S(2)}) collective-permute-start(bf16[512,512]{1,0:T(8,128)(2,1)S(1)} %copy-done.3), channel_id=1, source_target_pairs={{0,4},{4,0},{1,5},{5,1},{2,6},{6,2},{3,7},{7,3}} | collective-permute-start | bytes 1572872 | tf_op jit(solution)/shard_map/ppermute | solution.py:559
  1823.3 152.9 %collective-permute-start.61 = (bf16[512,512]{1,0:T(8,128)(2,1)S(1)}, bf16[512,512]{1,0:T(8,128)(2,1)}, u32[]{:S(2)}, u32[]{:S(2)}) collective-permute-start(bf16[512,512]{1,0:T(8,128)(2,1)S(1)} %collective-permute-done.57.refs_2_), channel_id=1, source_target_pairs={{0,4},{4,0},{1,5},{5,1},{2,6},{6,2},{3,7},{7,3}} | collective-permute-start | bytes 1572872 | tf_op jit(solution)/shard_map/ppermute | solution.py:559
  1824.8 151.5 %collective-permute-start.62 = (bf16[512,512]{1,0:T(8,128)(2,1)}, bf16[512,512]{1,0:T(8,128)(2,1)}, u32[]{:S(2)}, u32[]{:S(2)}) collective-permute-start(bf16[512,512]{1,0:T(8,128)(2,1)} %collective-permute-done.58.refs_3_), channel_id=1, source_target_pairs={{0,4},{4,0},{1,5},{5,1},{2,6},{6,2},{3,7},{7,3}} | collective-permute-start | bytes 1572872 | tf_op jit(solution)/shard_map/ppermute | solution.py:559
  1825.4 150.9 %collective-permute-start.63 = (bf16[512,512]{1,0:T(8,128)(2,1)}, bf16[512,512]{1,0:T(8,128)(2,1)}, u32[]{:S(2)}, u32[]{:S(2)}) collective-permute-start(bf16[512,512]{1,0:T(8,128)(2,1)} %collective-permute-done.59.refs_4_), channel_id=1, source_target_pairs={{0,4},{4,0},{1,5},{5,1},{2,6},{6,2},{3,7},{7,3}} | collective-permute-start | bytes 1572872 | tf_op jit(solution)/shard_map/ppermute | solution.py:559
  1966.4 176.2 %collective-permute-start.56 = (f32[256,3840]{1,0:T(8,128)}, f32[256,3840]{1,0:T(8,128)}, u32[]{:S(2)}, u32[]{:S(2)}) collective-permute-start(f32[256,3840]{1,0:T(8,128)} %get-tuple-element.136), channel_id=1, source_target_pairs={{0,4},{4,0},{1,5},{5,1},{2,6},{6,2},{3,7},{7,3}} | collective-permute-start | bytes 11796488 | tf_op jit(solution)/shard_map/ppermute | solution.py:559
  1975.7 168.3 %collective-permute-start.55 = (bf16[256,3840]{1,0:T(8,128)(2,1)}, bf16[256,3840]{1,0:T(8,128)(2,1)}, u32[]{:S(2)}, u32[]{:S(2)}) collective-permute-start(bf16[256,3840]{1,0:T(8,128)(2,1)} %get-tuple-element.135.refs_21_), channel_id=1, source_target_pairs={{0,4},{4,0},{1,5},{5,1},{2,6},{6,2},{3,7},{7,3}} | collective-permute-start | bytes 5898248 | tf_op jit(solution)/shard_map/ppermute | solution.py:559
  2115.5 163.8 %collective-permute-start.64 = (f32[256,3840]{1,0:T(8,128)}, f32[256,3840]{1,0:T(8,128)}, u32[]{:S(2)}, u32[]{:S(2)}) collective-permute-start(f32[256,3840]{1,0:T(8,128)} %get-tuple-element.147), channel_id=1, source_target_pairs={{0,4},{4,0},{1,5},{5,1},{2,6},{6,2},{3,7},{7,3}} | collective-permute-start | bytes 11796488 | tf_op jit(solution)/shard_map/ppermute | solution.py:559
  2214.9 209.0 %collective-permute-start.66 = (bf16[256,3840]{1,0:T(8,128)(2,1)}, bf16[256,3840]{1,0:T(8,128)(2,1)}, u32[]{:S(2)}, u32[]{:S(2)}) collective-permute-start(bf16[256,3840]{1,0:T(8,128)(2,1)} %get-tuple-element.145.refs_3_), channel_id=1, source_target_pairs={{0,4},{4,0},{1,5},{5,1},{2,6},{6,2},{3,7},{7,3}} | collective-permute-start | bytes 5898248 | tf_op jit(solution)/shard_map/ppermute | solution.py:559
  (64 other events, 4092.4 us)
